TPU v7x, 32 devices: a whole 2x2x4 slice. The times are simulated.
32 devices in a mesh: clump: 8 (over z, y), grp: 4 (over x, core).
Axes of the slice: x: 2, y: 2, z: 4, core: 2. Of those that a mesh axis runs over, the one named last changes fastest.
Arguments:
- flux: float32 [32, 1024, 64], P(('clump', 'grp')), may hold values from -6 to 6
- patch_pft: int32 [32, 1024], P(('clump', 'grp')), may hold values from 0 to 15
- patch_wt: float32 [32, 1024], P(('clump', 'grp')), may hold values from 0.2 to 2
- patch_col: int32 [32, 1024], P(('clump', 'grp')), may hold values from 0 to 511, never falling along the last dimension, each value on 1 to 4 neighbouring positions
- col_wt: float32 [32, 512], P(('clump', 'grp')), may hold values from 0.2 to 2
- col_lu: int32 [32, 512], P(('clump', 'grp')), may hold values from 0 to 255, never falling along the last dimension, each value on 1 to 4 neighbouring positions
- lu_wt: float32 [32, 256], P(('clump', 'grp')), may hold values from 0.2 to 2
- lu_grid: int32 [32, 256], P(('clump', 'grp')), may hold values from 0 to 127, never falling along the last dimension, each value on 1 to 4 neighbouring positions
- cell_target: int32 [32, 128], P(('clump', 'grp')), may hold values from 0 to 4095, as said below
- patch_count: int32 [32], P(('clump', 'grp')), may hold values from 64 to 1024
- pft_scale: float32 [16, 64], replicated, may hold values from 0.3 to 3
- cpl_frac: float32 [4096], P(('clump', 'grp')), may hold values from 0.2 to 0.9
- cpl_field: float32 [4096, 64], P(('clump', 'grp')), may hold values from -6 to 6
Outputs:
- grid_merged: float32 [4096, 64], P(('clump', 'grp'))
- anomaly: float32 [32, 1024, 64], P(('clump', 'grp'))
Inputs may be any that keep to these rules, and one draw needn't show every extreme that they name: `patch_col`: within each device's row the column numbers never fall, and each column holds 1 to 4 patch slots. `col_lu`: within each device's row the landunit numbers never fall, and each landunit holds 1 to 4 columns. `lu_grid`: within each device's row the gridcell numbers never fall, and each gridcell holds 1 to 4 landunits. `cell_target`: all devices' entries together are a permutation of 0 to 4095; the coupler owner of an entry q is q // 128, and each device's 128 gridcells go to 16 owners, exactly 8 to each.
All inputs are finite; a program needn't handle non-finite values.
Results may differ from a plain program's by a relative error of at most 0.0003.
Values sent between devices are 32-bit elements; how exact they have to be, the bound alone decides.
A program may use at most 64 MiB of HBM per device.

v0:
```python
import jax
import jax.numpy as jnp
from jax import lax
from jax.sharding import PartitionSpec as P

HIGH = lax.Precision.HIGHEST


def window_pick(padded, start, relative, width):
    window = lax.dynamic_slice_in_dim(padded, start, width, 0)
    onehot = (relative[:, None] == jnp.arange(width, dtype=jnp.int32)[None, :]).astype(jnp.float32)
    return jnp.dot(onehot, window, precision=HIGH)


def per_device(
    flux,
    patch_pft,
    patch_wt,
    patch_col,
    col_wt,
    col_lu,
    lu_wt,
    lu_grid,
    cell_target,
    patch_count,
    pft_scale,
    cpl_frac,
    cpl_field,
):
    n_clump = lax.axis_size("clump")
    n_group = lax.axis_size("grp")
    n_devices = n_clump * n_group
    values = flux[0]
    patches = values.shape[0]
    width_vars = values.shape[1]
    cell_count = cell_target.shape[1]
    capacity = max(2, 2 * cell_count // n_devices)
    slot_total = n_devices * capacity
    block = min(512, patches)
    blocks = patches // block
    position = jnp.arange(patches, dtype=jnp.int32)
    alive_mask = (position < patch_count[0]).astype(jnp.float32)
    type_onehot = (
        patch_pft[0][:, None] == jnp.arange(pft_scale.shape[0], dtype=jnp.int32)[None, :]
    ).astype(jnp.float32)
    scaled = values * jnp.dot(type_onehot, pft_scale, precision=HIGH)
    col_table = jnp.stack([col_wt[0], col_lu[0].astype(jnp.float32)], axis=1)
    col_table = jnp.concatenate([col_table, jnp.zeros((block, 2), jnp.float32)], axis=0)
    lu_table = jnp.stack([lu_wt[0], lu_grid[0].astype(jnp.float32)], axis=1)
    lu_table = jnp.concatenate([lu_table, jnp.zeros((block, 2), jnp.float32)], axis=0)
    within = jnp.arange(block, dtype=jnp.int32)

    def gather_block(carry, entries):
        num_acc, den_acc = carry
        cols_blk, alive_blk, pwt_blk, scaled_blk = entries
        col_start = cols_blk[0]
        col_vals = window_pick(col_table, col_start, cols_blk - col_start, block)
        land_blk = col_vals[:, 1].astype(jnp.int32)
        land_start = land_blk[0]
        lu_vals = window_pick(lu_table, land_start, land_blk - land_start, block)
        home_blk = lu_vals[:, 1].astype(jnp.int32)
        weight_blk = alive_blk * pwt_blk * col_vals[:, 0] * lu_vals[:, 0]
        home_start = home_blk[0]
        cell_onehot = (within[:, None] == (home_blk - home_start)[None, :]).astype(jnp.float32)
        part_num = jnp.dot(cell_onehot, scaled_blk * weight_blk[:, None], precision=HIGH)
        part_den = jnp.dot(cell_onehot, weight_blk, precision=HIGH)
        old_num = lax.dynamic_slice_in_dim(num_acc, home_start, block, 0)
        old_den = lax.dynamic_slice_in_dim(den_acc, home_start, block, 0)
        num_acc = lax.dynamic_update_slice_in_dim(num_acc, old_num + part_num, home_start, 0)
        den_acc = lax.dynamic_update_slice_in_dim(den_acc, old_den + part_den, home_start, 0)
        return ((num_acc, den_acc), home_blk)

    start_acc = (
        jnp.zeros((cell_count + block, width_vars), jnp.float32),
        jnp.zeros((cell_count + block,), jnp.float32),
    )
    block_inputs = (
        patch_col[0].reshape(blocks, block),
        alive_mask.reshape(blocks, block),
        patch_wt[0].reshape(blocks, block),
        scaled.reshape(blocks, block, width_vars),
    )
    (num_acc, den_acc), home_blocks = lax.scan(gather_block, start_acc, block_inputs)
    cell_num = num_acc[:cell_count]
    cell_den = den_acc[:cell_count]
    target = cell_target[0]
    owner_dev = target // cell_count
    local_slot = target - owner_dev * cell_count
    same_owner = (owner_dev[:, None] == owner_dev[None, :]).astype(jnp.int32)
    earlier = (
        jnp.arange(cell_count, dtype=jnp.int32)[None, :]
        < jnp.arange(cell_count, dtype=jnp.int32)[:, None]
    ).astype(jnp.int32)
    rank_within = jnp.sum(same_owner * earlier, axis=1)
    slot = owner_dev * capacity + rank_within
    slot_onehot = (jnp.arange(slot_total, dtype=jnp.int32)[:, None] == slot[None, :]).astype(
        jnp.float32
    )
    slot_used = jnp.sum(slot_onehot, axis=1)
    send_slot = jnp.dot(slot_onehot, local_slot.astype(jnp.float32), precision=HIGH) + (
        1.0 - slot_used
    ) * float(cell_count)
    send_slot = send_slot.reshape(n_clump, n_group, capacity)
    cell_mean = cell_num / jnp.maximum(cell_den, 1.0)[:, None]
    send_mean = jnp.dot(slot_onehot, cell_mean, precision=HIGH)
    outgoing = (send_mean.reshape(n_clump, n_group, capacity, width_vars), send_slot)
    incoming = (
        lax.all_to_all(
            lax.all_to_all(outgoing[0], "clump", split_axis=0, concat_axis=0, tiled=True),
            "grp",
            split_axis=1,
            concat_axis=1,
            tiled=True,
        ),
        lax.all_to_all(
            lax.all_to_all(outgoing[1], "clump", split_axis=0, concat_axis=0, tiled=True),
            "grp",
            split_axis=1,
            concat_axis=1,
            tiled=True,
        ),
    )
    slot_ids = incoming[-1].reshape(-1).astype(jnp.int32)
    owner_onehot = (slot_ids[:, None] == jnp.arange(cell_count, dtype=jnp.int32)[None, :]).astype(
        jnp.float32
    )
    owned_mean = jnp.dot(owner_onehot.T, incoming[0].reshape(-1, width_vars), precision=HIGH)
    grid_merged = cpl_frac[:, None] * owned_mean + (1.0 - cpl_frac)[:, None] * cpl_field
    reply_rows = jnp.dot(owner_onehot, grid_merged, precision=HIGH).reshape(
        n_clump, n_group, capacity, width_vars
    )
    returned = lax.all_to_all(
        lax.all_to_all(reply_rows, "clump", split_axis=0, concat_axis=0, tiled=True),
        "grp",
        split_axis=1,
        concat_axis=1,
        tiled=True,
    )
    cell_merged = jnp.dot(slot_onehot.T, returned.reshape(slot_total, width_vars), precision=HIGH)
    merged_table = jnp.concatenate(
        [cell_merged, jnp.zeros((block, width_vars), jnp.float32)], axis=0
    )

    def spread_block(entries):
        home_blk, alive_blk, scaled_blk = entries
        home_start = home_blk[0]
        picked = window_pick(merged_table, home_start, home_blk - home_start, block)
        return alive_blk[:, None] * (scaled_blk - picked)

    anomaly = lax.map(
        spread_block,
        (home_blocks, alive_mask.reshape(blocks, block), scaled.reshape(blocks, block, width_vars)),
    )
    return (grid_merged, anomaly.reshape(1, patches, width_vars))


def solution(mesh):
    return jax.shard_map(
        per_device,
        mesh=mesh,
        in_specs=(
            P(("clump", "grp"), None, None),
            P(("clump", "grp"), None),
            P(("clump", "grp"), None),
            P(("clump", "grp"), None),
            P(("clump", "grp"), None),
            P(("clump", "grp"), None),
            P(("clump", "grp"), None),
            P(("clump", "grp"), None),
            P(("clump", "grp"), None),
            P(("clump", "grp")),
            P(),
            P(("clump", "grp")),
            P(("clump", "grp"), None),
        ),
        out_specs=(P(("clump", "grp"), None), P(("clump", "grp"), None, None)),
        check_vma=False,
    )
```

profile of v0, /device:TPU:0, one launch (start us, length us, event | category | flops | bytes accessed | tf_op | source)
XLA Modules:
  0.0 106.9 jit_solution(788008277498538944)
XLA Ops:
  0.7 0.7 and_select_fusion
  1.9 0.7 reshape.154
  2.6 7.4 %all-to-all-start = ((f32[8,4,8]{2,1,0:T(4,128)}), f32[8,4,8]{2,1,0:T(4,128)S(1)}, u32[]{:S(2)}, u32[]{:S(2)}) async-start(f32[8,4,8]{2,1,0:T(4,128)} %reshape.154), calls=%async_computation | async-start | bytes 32768 | tf_op jit(solution)/shard_map/all_to_all | solution.py:116
  10.1 1.5 %convolution_multiply_fusion = f32[1024,64]{0,1:T(8,128)S(1)} fusion(f32[16,64]{1,0:T(8,128)S(1)} %copy-done, f32[1,1024,64]{1,2,0:T(8,128)} %param.17, s32[1024]{0:T(1024)S(1)} %bitcast.148), kind=kOutput, calls=%fused_computation.43 | convolution fusion | flops 12664832 | bytes 532480 | tf_op jit(solution)/shard_map/dot_general | solution.py:46
  12.5 0.7 copy-done.6
  13.9 0.6 reduce.6
  15.2 0.6 reduce.7
  15.9 0.7 copy-done.8
  16.5 0.7 copy-done.7
  17.2 0.7 copy-done.9
  17.9 26.6 %while.26 = (s32[]{:T(128)}, f32[640,64]{0,1:T(8,128)S(1)}, f32[640]{0:T(1024)S(1)}, s32[2,512]{1,0:T(2,128)S(1)}, s32[2,512]{1,0:T(2,128)S(1)}, /*index=5*/f32[...) while((s32[]{:T(128)}, f32[640,64]{0,1:T(8,128)S(1)}, ...), condition=%wide.region_3.4_spmd.clone, body=%wide.region_2.3_spmd.clone.sunk | while | flops 218176016 | bytes 1268031 | solution.py:83
  20.4 0.6 dynamic-slice_subtract_fusion.5
  21.1 0.6 fusion.62
  24.2 0.6 broadcast_subtract_fusion.5
  27.9 0.6 broadcast_subtract_fusion.6
  28.8 0.7 convolution_add_fusion.2
  29.6 0.8 dynamic_update_slice.24
  33.6 0.6 dynamic-slice_subtract_fusion.5
  37.4 0.6 broadcast_subtract_fusion.5
  38.0 0.6 fusion.63
  41.2 0.6 broadcast_subtract_fusion.6
  42.1 0.8 convolution_add_fusion.2
  42.8 1.0 dynamic_update_slice.24
  44.8 0.8 reshape.183
  45.6 6.0 %all-to-all-start.2 = ((f32[8,1,2048]{2,1,0:T(1,128)}), f32[8,1,2048]{2,1,0:T(1,128)S(1)}, u32[]{:S(2)}, u32[]{:S(2)}) async-start(f32[8,1,2048]{2,1,0:T(1,128)} %reshape.183), calls=%async_computation.2 | async-start | bytes 131072 | tf_op jit(solution)/shard_map/all_to_all | solution.py:109
  52.2 6.3 %all-to-all-done.2 = f32[8,1,2048]{2,1,0:T(1,128)S(1)} async-done(((f32[8,1,2048]{2,1,0:T(1,128)}), f32[8,1,2048]{2,1,0:T(1,128)S(1)}, u32[]{:S(2)}, u32[]{:S(2)}) %all-to-all-start.2) | async-done | bytes 65568 | tf_op jit(solution)/shard_map/all_to_all | solution.py:109
  58.5 3.3 %all-to-all-start.1 = ((f32[8,4,8]{2,0,1:T(8,128)}), f32[8,4,8]{2,0,1:T(8,128)S(1)}, u32[]{:S(2)}, u32[]{:S(2)}) async-start(f32[8,4,8]{2,0,1:T(8,128)} %copy.47), calls=%async_computation.1 | async-start | bytes 32768 | tf_op jit(solution)/shard_map/all_to_all | solution.py:115
  62.3 0.8 reduce.8
  63.2 0.8 reshape.185
  64.0 1.6 %all-to-all-done.1 = f32[8,4,8]{2,0,1:T(8,128)S(1)} async-done(((f32[8,4,8]{2,0,1:T(8,128)}), f32[8,4,8]{2,0,1:T(8,128)S(1)}, u32[]{:S(2)}, u32[]{:S(2)}) %all-to-all-start.1) | async-done | bytes 1056 | tf_op jit(solution)/shard_map/all_to_all | solution.py:115
  65.6 3.3 %all-to-all-start.3 = ((f32[4,1,4096]{2,1,0:T(1,128)}), f32[4,1,4096]{2,1,0:T(1,128)S(1)}, u32[]{:S(2)}, u32[]{:S(2)}) async-start(f32[4,1,4096]{2,1,0:T(1,128)} %reshape.185), calls=%async_computation.3 | async-start | bytes 131072 | tf_op jit(solution)/shard_map/all_to_all | solution.py:108
  69.0 3.9 %all-to-all-done.3 = f32[4,1,4096]{2,1,0:T(1,128)S(1)} async-done(((f32[4,1,4096]{2,1,0:T(1,128)}), f32[4,1,4096]{2,1,0:T(1,128)S(1)}, u32[]{:S(2)}, u32[]{:S(2)}) %all-to-all-start.3) | async-done | bytes 65568 | tf_op jit(solution)/shard_map/all_to_all | solution.py:108
  72.9 0.8 reduce.9
  73.9 0.7 copy-done.2
  75.7 9.3 %all_to_all.30 = f32[8,1,2048]{2,1,0:T(1,128)S(1)} all-to-all(f32[8,1,2048]{2,1,0:T(1,128)S(1)} %reshape.187), channel_id=1, replica_groups=mesh['clump'=8,'grp'=4] {'clump'}, dimensions={0} | all-to-all | bytes 131072 | tf_op jit(solution)/shard_map/all_to_all | solution.py:133
  85.0 0.8 reduce.10
  85.9 0.8 reshape.189
  86.6 3.3 %all-to-all-start.5 = ((f32[4,1,4096]{2,1,0:T(1,128)}), f32[4,1,4096]{2,1,0:T(1,128)S(1)}, u32[]{:S(2)}, u32[]{:S(2)}) async-start(f32[4,1,4096]{2,1,0:T(1,128)} %reshape.189), calls=%async_computation.5 | async-start | bytes 131072 | tf_op jit(solution)/shard_map/all_to_all | solution.py:132
  89.9 4.1 %all-to-all-done.5 = f32[4,1,4096]{2,1,0:T(1,128)S(1)} async-done(((f32[4,1,4096]{2,1,0:T(1,128)}), f32[4,1,4096]{2,1,0:T(1,128)S(1)}, u32[]{:S(2)}, u32[]{:S(2)}) %all-to-all-start.5) | async-done | bytes 65568 | tf_op jit(solution)/shard_map/all_to_all | solution.py:132
  94.0 0.8 reduce.11
  95.3 10.7 %while.25 = (s32[]{:T(128)}, f32[2,512,64]{1,0,2:T(2,128)S(1)}, f32[2,512]{1,0:T(2,128)S(1)}, f32[2,512,64]{1,0,2:T(2,128)S(1)}, s32[2,512]{1,0:T(2,128)S(1)}, /...) while((s32[]{:T(128)}, f32[2,512,64]{1,0,2:T(2,128)S(1)}, f32[2,512]{1,0:T(2,128)S(1)}, ...), condition=%wide.region_5.6_spmd, body=%wide.region_4.5_spmd.sunk | while | flops 201654784 | bytes 1192099 | solution.py:150
  97.7 0.7 dynamic-slice_subtract_fusion.4
  98.5 0.7 fusion.58
  99.4 1.2 %dynamic_update_slice.22 = f32[2,512,64]{1,0,2:T(2,128)S(1)} dynamic-update-slice(f32[2,512,64]{1,0,2:T(2,128)S(1)} %get-tuple-element.402, f32[1,512,64]{1,0,2:T(1,128)S(1)} %copy.81, s32[]{:T(128)} %get-tuple-element.401, s32[]{:T(128)} %constant.46.clone.1..sunk, s32[]{:T(128)} %constant.46.clone.1..sunk) | dynamic-update-slice | bytes 262148 | tf_op jit(solution)/shard_map/while/body/jit(dynamic_update_index_in_dim)/dynamic_update_slice | solution.py:150
  103.1 0.7 dynamic-slice_subtract_fusion.4
  103.9 0.7 fusion.58
  104.8 1.2 %dynamic_update_slice.22 = f32[2,512,64]{1,0,2:T(2,128)S(1)} dynamic-update-slice(f32[2,512,64]{1,0,2:T(2,128)S(1)} %get-tuple-element.402, f32[1,512,64]{1,0,2:T(1,128)S(1)} %copy.81, s32[]{:T(128)} %get-tuple-element.401, s32[]{:T(128)} %constant.46.clone.1..sunk, s32[]{:T(128)} %constant.46.clone.1..sunk) | dynamic-update-slice | bytes 262148 | tf_op jit(solution)/shard_map/while/body/jit(dynamic_update_index_in_dim)/dynamic_update_slice | solution.py:150
  106.0 0.9 reshape.160
  (93 shorter events, 13.7 us)
Async XLA Ops:
  0.6 9.4 %copy-start = (f32[16,64]{1,0:T(8,128)S(1)}, f32[16,64]{1,0:T(8,128)}, u32[]{:S(2)}) copy-start(f32[16,64]{1,0:T(8,128)} %param.27) | copy-start | bytes 12292
  0.6 0.7 copy-start.11
  2.6 7.5 %copy-start.3 = (s32[1,1024]{1,0:T(1,128)S(1)}, s32[1,1024]{1,0:T(1,128)}, u32[]{:S(2)}) copy-start(s32[1,1024]{1,0:T(1,128)} %param.18) | copy-start | bytes 12292
  2.6 42.9 %all-to-all-start = ((f32[8,4,8]{2,1,0:T(4,128)}), f32[8,4,8]{2,1,0:T(4,128)S(1)}, u32[]{:S(2)}, u32[]{:S(2)}) async-start(f32[8,4,8]{2,1,0:T(4,128)} %reshape.154), calls=%async_computation | async-start | bytes 32768 | tf_op jit(solution)/shard_map/all_to_all | solution.py:116
  12.5 0.7 copy-start.6
  13.2 0.7 copy-start.4
  14.5 0.7 copy-start.5
  15.9 0.7 copy-start.8
  16.5 0.7 copy-start.7
  17.2 0.7 copy-start.9
  45.6 12.9 %all-to-all-start.2 = ((f32[8,1,2048]{2,1,0:T(1,128)}), f32[8,1,2048]{2,1,0:T(1,128)S(1)}, u32[]{:S(2)}, u32[]{:S(2)}) async-start(f32[8,1,2048]{2,1,0:T(1,128)} %reshape.183), calls=%async_computation.2 | async-start | bytes 131072 | tf_op jit(solution)/shard_map/all_to_all | solution.py:109
  58.5 7.1 %all-to-all-start.1 = ((f32[8,4,8]{2,0,1:T(8,128)}), f32[8,4,8]{2,0,1:T(8,128)S(1)}, u32[]{:S(2)}, u32[]{:S(2)}) async-start(f32[8,4,8]{2,0,1:T(8,128)} %copy.47), calls=%async_computation.1 | async-start | bytes 32768 | tf_op jit(solution)/shard_map/all_to_all | solution.py:115
  64.0 4.9 %copy-start.10 = (f32[128]{0:T(128)S(1)}, f32[128]{0:T(128)}, u32[]{:S(2)}) copy-start(f32[128]{0:T(128)} %param.28) | copy-start | bytes 1540
  65.6 7.4 %all-to-all-start.3 = ((f32[4,1,4096]{2,1,0:T(1,128)}), f32[4,1,4096]{2,1,0:T(1,128)S(1)}, u32[]{:S(2)}, u32[]{:S(2)}) async-start(f32[4,1,4096]{2,1,0:T(1,128)} %reshape.185), calls=%async_computation.3 | async-start | bytes 131072 | tf_op jit(solution)/shard_map/all_to_all | solution.py:108
  73.9 0.8 copy-start.2
  75.0 0.6 copy-start.1
  86.6 7.4 %all-to-all-start.5 = ((f32[4,1,4096]{2,1,0:T(1,128)}), f32[4,1,4096]{2,1,0:T(1,128)S(1)}, u32[]{:S(2)}, u32[]{:S(2)}) async-start(f32[4,1,4096]{2,1,0:T(1,128)} %reshape.189), calls=%async_computation.5 | async-start | bytes 131072 | tf_op jit(solution)/shard_map/all_to_all | solution.py:132
where the time goes:
time: 108 us; the launch traced here: 107 us
  starting transfers between devices  23.3 us (22%)
  local copies, waits for them, and re-layouts  20.7 us (19%)
  waiting for transfers between devices  15.9 us (15%)
  loops' own time  15.6 us (14%)
  other arithmetic  11.2 us (10%)
  blocking collectives  9.29 us (9%)
  matrix products  9.28 us (9%)
  between operations  1.59 us (1%)
    another operation x1, loops' own time, per_device(): lax.scan(gather_block, start_acc, block_inputs)  11.6 us
    all_to_all x1, blocking collectives, per_device(): lax.all_to_all(reply_rows, 'clump', split_axis=0, concat_axis=0, tiled=True)  9.29 us
    unnamed x34, local copies, waits for them, and re-layouts  7.96 us
    all_to_all x1, starting transfers between devices, per_device(): lax.all_to_all(outgoing[1], 'clump', split_axis=0, concat_axis=0, tiled=T...  7.44 us
    all_to_all x1, waiting for transfers between devices, per_device(): lax.all_to_all(outgoing[0], 'clump', split_axis=0, concat_axis=0, tiled=T...  6.3 us
    all_to_all x1, starting transfers between devices, per_device(): lax.all_to_all(outgoing[0], 'clump', split_axis=0, concat_axis=0, tiled=T...  5.99 us
    all_to_all x1, waiting for transfers between devices, per_device(): lax.all_to_all(lax.all_to_all(reply_rows, 'clump', split_axis=0, concat_a...  4.08 us
    another operation x1, loops' own time, per_device(): lax.map(spread_block, (home_blocks, alive_mask.reshape(blocks, block), sc...  3.99 us
  transfers between devices with their start and end apart: 5, of which 4 were waited for; matrix products, arithmetic and copies ran while one was open for 22% of the time, Pallas kernels for 0%

commit v1 on v0

v1 whole, which is shorter than its diff:
```python
import functools

import jax
import jax.numpy as jnp
from jax import lax
from jax.experimental import pallas as pl
from jax.experimental.pallas import tpu as pltpu
from jax.sharding import PartitionSpec as P

MESH = pl.DeviceIdType.MESH
F32 = jnp.float32
BF16 = jnp.bfloat16


def iota(shape, dim):
    return lax.broadcasted_iota(jnp.int32, shape, dim)


def onehot(mask):
    return jnp.where(mask, 1.0, 0.0).astype(BF16)


def halves(x):
    high = x.astype(BF16)
    return high, (x - high.astype(F32)).astype(BF16)


def dot(a, b):
    return jnp.dot(a, b, preferred_element_type=F32)


def dot_nt(a, b):
    return lax.dot_general(a, b, (((1,), (1,)), ((), ())), preferred_element_type=F32)


def rows_of(rows, total):
    n = rows[0].shape[1]
    at = iota((total, n), 0)
    out = jnp.zeros((total, n), F32)
    for k, row in enumerate(rows):
        out = jnp.where(at == k, jnp.broadcast_to(row.astype(F32), (total, n)), out)
    return out.astype(BF16)


def kernel(
    n_clump, n_group, cap,
    count_ref, flux_ref, pft_ref, pwt_ref, pcol_ref, cwt_ref, clu_ref, lwt_ref, lgrid_ref,
    target_ref, scale_ref, frac_ref, field_ref,
    merged_ref, anomaly_ref,
    send, recv, reply, back, send_sem, recv_sem,
):
    n = n_clump * n_group
    me = lax.axis_index("clump") * n_group + lax.axis_index("grp")

    def device(index):
        return (index // n_group, index % n_group)

    barrier = pltpu.get_barrier_semaphore()

    def greet(j, carry):
        pl.semaphore_signal(
            barrier, inc=1, device_id=device((me + j) % n), device_id_type=MESH
        )
        return carry

    lax.fori_loop(1, n, greet, 0)

    nv, patches = flux_ref.shape
    types = scale_ref.shape[0]
    cols = cwt_ref.shape[1]
    lus = lwt_ref.shape[1]
    cells = target_ref.shape[1]
    slots = n * cap

    lu_hi, lu_lo = halves(lwt_ref[...])
    lu_rows = rows_of([lu_hi, lu_lo, lgrid_ref[...]], 16)
    lu_of = onehot(iota((lus, cols), 0) == clu_ref[...])
    col_vals = dot(lu_rows, lu_of)
    col_w = cwt_ref[...] * (col_vals[0:1] + col_vals[1:2])
    c_hi, c_lo = halves(col_w)
    col_rows = rows_of([c_hi, c_lo, col_vals[2:3]], 16)
    col_of = onehot(iota((cols, patches), 0) == pcol_ref[...])
    patch_vals = dot(col_rows, col_of)
    alive = jnp.where(iota((1, patches), 1) < count_ref[0], 1.0, 0.0)
    weight = alive * pwt_ref[...] * (patch_vals[0:1] + patch_vals[1:2])
    home = patch_vals[2:3].astype(jnp.int32)
    home_of = onehot(iota((cells, patches), 0) == home)

    table = scale_ref[...]
    t1 = table.astype(BF16).astype(F32)
    t2 = (table - t1).astype(BF16).astype(F32)
    t3 = table - t1 - t2
    pad = 128 - 3 * types
    stacked = jnp.concatenate([t1, t2, t3, jnp.zeros((pad, nv), F32)], axis=0)
    stacked = jnp.concatenate([stacked, jnp.zeros((128, 128 - nv), F32)], axis=1)
    scale_t = stacked.T[:nv].astype(BF16)
    kind = iota((128, patches), 0)
    type_of = onehot(
        (kind == pft_ref[...])
        | (kind == pft_ref[...] + types)
        | (kind == pft_ref[...] + 2 * types)
    )
    scaled = flux_ref[...] * dot(scale_t, type_of)

    x_hi, x_lo = halves(scaled * weight)
    w_hi, w_lo = halves(weight)
    sums = dot_nt(
        jnp.concatenate([x_hi, x_lo, rows_of([w_hi, w_lo], 16)], axis=0), home_of
    )
    num = sums[:nv] + sums[nv : 2 * nv]
    den = sums[2 * nv : 2 * nv + 1] + sums[2 * nv + 1 : 2 * nv + 2]
    mean = num / jnp.maximum(den, 1.0)

    target = target_ref[...]
    owner = target // cells
    local = target - owner * cells
    owner_b = jnp.broadcast_to(owner.astype(F32), (cells, cells))
    same = owner_b == owner_b.T
    earlier = iota((cells, cells), 0) < iota((cells, cells), 1)
    rank = jnp.sum(jnp.where(same & earlier, 1.0, 0.0), axis=0, keepdims=True).astype(jnp.int32)
    ahead = owner - me
    ahead = jnp.where(ahead < 0, ahead + n, ahead)
    slot = ahead * cap + rank
    slot_of = onehot(iota((slots, cells), 0) == slot)

    m_hi, m_lo = halves(mean)
    pad_rows = 128 - nv
    ids = rows_of([local + 1], pad_rows)
    left = jnp.concatenate([m_hi, ids], axis=0)
    right = jnp.concatenate([m_lo, jnp.zeros((pad_rows, cells), BF16)], axis=0)
    send[...] = dot_nt(slot_of, left) + dot_nt(slot_of, right)
    recv[0:cap, :] = send[0:cap, :]

    pl.semaphore_wait(barrier, n - 1)

    def copy(source, into, k, j, where):
        rows = pl.ds(pl.multiple_of(j * cap, cap), cap)
        return pltpu.make_async_remote_copy(
            src_ref=source.at[rows],
            dst_ref=into.at[rows],
            send_sem=send_sem.at[k],
            recv_sem=recv_sem.at[k],
            device_id=device(where),
            device_id_type=MESH,
        )

    def forth(j, carry):
        copy(send, recv, 0, j, (me + j) % n).start()
        return carry

    def home_again(j, carry):
        copy(reply, back, 1, j, (me + n - j) % n).start()
        return carry

    def wait(buffer, sem):
        rest = buffer.at[pl.ds(cap, slots - cap)]
        pltpu.make_async_copy(rest, rest, sem).wait()

    lax.fori_loop(1, n, forth, 0)
    wait(recv, recv_sem.at[0])

    got = recv[...]
    got_ids = got[:, nv : nv + 1].astype(jnp.int32)
    owned_of = onehot(iota((slots, cells), 1) + 1 == got_ids)
    g_hi, g_lo = halves(got.T[:nv])
    both = dot(jnp.concatenate([g_hi, g_lo], axis=0), owned_of)
    frac = frac_ref[...]
    merged = frac * (both[:nv] + both[nv:]) + (1.0 - frac) * field_ref[...]
    merged_ref[...] = merged
    r_hi, r_lo = halves(merged)
    blank = jnp.zeros((pad_rows, cells), BF16)
    reply[...] = dot_nt(owned_of, jnp.concatenate([r_hi, blank], axis=0)) + dot_nt(
        owned_of, jnp.concatenate([r_lo, blank], axis=0)
    )
    back[0:cap, :] = reply[0:cap, :]
    lax.fori_loop(1, n, home_again, 0)
    wait(back, recv_sem.at[1])

    b_hi, b_lo = halves(back[...].T[:nv])
    cell = dot(jnp.concatenate([b_hi, b_lo], axis=0), slot_of)
    c_hi, c_lo = halves(cell[:nv] + cell[nv:])
    picked = dot(jnp.concatenate([c_hi, c_lo], axis=0), home_of)
    anomaly_ref[...] = alive * (scaled - (picked[:nv] + picked[nv:]))
    wait(send, send_sem.at[0])
    wait(reply, send_sem.at[1])


def per_device(
    flux, patch_pft, patch_wt, patch_col, col_wt, col_lu, lu_wt, lu_grid, cell_target,
    patch_count, pft_scale, cpl_frac, cpl_field,
):
    n_clump = lax.axis_size("clump")
    n_group = lax.axis_size("grp")
    n = n_clump * n_group
    nv = flux.shape[2]
    patches = flux.shape[1]
    cells = cell_target.shape[1]
    cap = max(2, 2 * cells // n)
    cap = -(-cap // 8) * 8
    vmem = pl.BlockSpec(memory_space=pltpu.VMEM)
    buffer = pltpu.VMEM((n * cap, 128), F32)
    merged, anomaly = pl.pallas_call(
        functools.partial(kernel, n_clump, n_group, cap),
        out_shape=(
            jax.ShapeDtypeStruct((nv, cells), F32),
            jax.ShapeDtypeStruct((nv, patches), F32),
        ),
        in_specs=[pl.BlockSpec(memory_space=pltpu.SMEM)] + [vmem] * 12,
        out_specs=(vmem, vmem),
        scratch_shapes=[
            buffer, buffer, buffer, buffer,
            pltpu.SemaphoreType.DMA((2,)),
            pltpu.SemaphoreType.DMA((2,)),
        ],
        compiler_params=pltpu.CompilerParams(collective_id=0, has_side_effects=True),
    )(
        patch_count, flux[0].T, patch_pft, patch_wt, patch_col, col_wt, col_lu, lu_wt,
        lu_grid, cell_target, pft_scale, cpl_frac.reshape(1, -1), cpl_field.T,
    )
    return merged.T, anomaly.T[None]


def solution(mesh):
    split = P(("clump", "grp"))
    return jax.shard_map(
        per_device,
        mesh=mesh,
        in_specs=(split,) * 10 + (P(),) + (split,) * 2,
        out_specs=(split, split),
        check_vma=False,
    )
```

time: 108 us -> 26.1 us (0.24)
  starting transfers between devices: 23.3 us -> 0 us
  Pallas kernels: 0 us -> 21.5 us
  local copies, waits for them, and re-layouts: 20.7 us -> 3.05 us
  waiting for transfers between devices: 15.9 us -> 0 us
  loops' own time: 15.6 us -> 0 us
  other arithmetic: 11.2 us -> 0 us
  blocking collectives: 9.29 us -> 0 us
  matrix products: 9.28 us -> 0 us
    all_to_all x5 -> x0, starting transfers between devices: 23.3 us -> none  [the longest x1 7.44 us: per_device(): lax.all_to_all(outgoing[1], 'clump', split_axis=0, concat_axis=0, tiled=T...]
    pallas_call x0 -> x1, Pallas kernels: none -> 21.5 us  [per_device(): pl.pallas_call(functools.partial(kernel, n_clump, n_group, cap), out_shap...]
    all_to_all x5 -> x0, waiting for transfers between devices: 15.9 us -> none  [the longest x1 6.3 us: per_device(): lax.all_to_all(outgoing[0], 'clump', split_axis=0, concat_axis=0, tiled=T...]
    another operation x2 -> x0, loops' own time: 15.6 us -> none  [the longest x1 11.6 us: per_device(): lax.scan(gather_block, start_acc, block_inputs)]
    all_to_all x1 -> x0, blocking collectives: 9.29 us -> none  [per_device(): lax.all_to_all(reply_rows, 'clump', split_axis=0, concat_axis=0, tiled=True)]
    dot_general x16 -> x0, matrix products: 9.28 us -> none  [the longest x6 3.97 us: window_pick(): return jnp.dot(onehot, window, precision=HIGH)]
    sub x9 -> x0, other arithmetic: 5.16 us -> none  [the longest x2 1.31 us: spread_block(): picked = window_pick(merged_table, home_start, home_blk - home_start, block)]
    unnamed x34 -> x2, local copies, waits for them, and re-layouts: 7.96 us -> 3.05 us
  transfers between devices with their start and end apart: 5 -> 0, of which waited for: 4 -> 0; matrix products, arithmetic and copies ran while one was open for 22% -> 0% of each run, Pallas kernels for 0% -> 0%
where the time goes in v1:
time: 26.1 us; the launch traced here: 25.8 us
  Pallas kernels  21.5 us (82%)
  local copies, waits for them, and re-layouts  3.05 us (12%)
  between operations  1.29 us (5%)
    pallas_call x1, Pallas kernels, per_device(): pl.pallas_call(functools.partial(kernel, n_clump, n_group, cap), out_shap...  21.5 us
    unnamed x2, local copies, waits for them, and re-layouts  3.05 us

profile of v1, /device:TPU:0, one launch (start us, length us, event | category | flops | bytes accessed | tf_op | source)
XLA Modules:
  0.0 25.8 jit_solution(17477529842774168103)
XLA Ops:
  1.3 21.5 %shard_map.140 = (f32[64,128]{1,0:T(8,128)}, f32[64,1024]{1,0:T(8,128)}) custom-call(s32[1]{0:T(128)S(6)} %copy.17.count_ref, f32[64,1024]{1,0:T(8,128)} %bitcast.9, s32[1,1024]{1,0:T(1,128)} %pft_ref.1, f32[1,1024]{1,0:T(1,128)} %pwt_ref.1, s32[1,1024]{1,0:T(1,128)} %pcol_ref.1, f32[1,512]{1,0:T(1,128)} %cwt_ref.1, s32[1,512]{1,0:T(1,128)} %clu_ref.1, ...), custom_call_target="tpu_custom_call" | custom-call | tf_op jit(solution)/shard_map/pallas_call | solution.py:202
  22.8 1.4 %copy.18 = f32[128,64]{0,1:T(8,128)} copy(f32[128,64]{0,1:T(8,128)} %bitcast.12) | data formatting | bytes 65536
  24.1 1.7 %copy.19 = f32[1,1024,64]{1,2,0:T(8,128)} copy(f32[1,1024,64]{1,2,0:T(8,128)} %bitcast.10) | data formatting | bytes 524288

commit v2 on v1

v2 whole, which is shorter than its diff:
```python
import functools

import jax
import jax.numpy as jnp
from jax import lax
from jax.experimental import pallas as pl
from jax.experimental.pallas import tpu as pltpu
from jax.sharding import PartitionSpec as P

MESH = pl.DeviceIdType.MESH
F32 = jnp.float32
BF16 = jnp.bfloat16
INPUTS = 12


def iota(shape, dim):
    return lax.broadcasted_iota(jnp.int32, shape, dim)


def onehot(mask):
    return jnp.where(mask, 1.0, 0.0).astype(BF16)


def halves(x):
    high = x.astype(BF16)
    return high, (x - high.astype(F32)).astype(BF16)


def dot(a, b):
    return jnp.dot(a, b, preferred_element_type=F32)


def dot_nt(a, b):
    return lax.dot_general(a, b, (((1,), (1,)), ((), ())), preferred_element_type=F32)


def rows_of(rows, total):
    n = rows[0].shape[1]
    at = iota((total, n), 0)
    out = jnp.zeros((total, n), F32)
    for k, row in enumerate(rows):
        out = jnp.where(at == k, jnp.broadcast_to(row.astype(F32), (total, n)), out)
    return out.astype(BF16)


def split_by(x, size):
    if size & (size - 1) == 0:
        return lax.shift_right_logical(x, jnp.int32(size.bit_length() - 1)), x & (size - 1)
    return x // size, x % size


def select(table, chosen):
    high, low = halves(table)
    both = dot(jnp.concatenate([high, low], axis=0), chosen)
    return both[: table.shape[0]] + both[table.shape[0] :]


def pack(chosen, x):
    rows = chosen.shape[0] // 2
    pair = jnp.concatenate([chosen[:rows], chosen[rows:]], axis=1)
    blank = jnp.zeros(x.shape, BF16)

    def wide(part):
        upper = jnp.concatenate([part, blank], axis=1)
        return jnp.concatenate([upper, jnp.concatenate([blank, part], axis=1)], axis=0)

    high, low = halves(x)
    return dot_nt(pair, wide(high)) + dot_nt(pair, wide(low))


def unpack(packed):
    turned = packed.T
    middle = turned.shape[0] // 2
    return jnp.concatenate([turned[:middle], turned[middle:]], axis=1)


def kernel(
    n_clump, n_group, cap, half, stride,
    *refs,
):
    count_ref, *refs = refs
    sources, refs = refs[:INPUTS], refs[INPUTS:]
    merged_ref, anomaly_ref = refs[:2]
    send, recv, reply, back, ask, asked, send_sem, recv_sem, in_sem = refs[2:11]
    staged = refs[11:]
    loads = [
        pltpu.make_async_copy(source, into, in_sem.at[k])
        for k, (source, into) in enumerate(zip(sources, staged))
    ]
    (
        target_ref, lwt_ref, lgrid_ref, clu_ref, cwt_ref, pcol_ref, pwt_ref,
        scale_ref, pft_ref, flux_ref, frac_ref, field_ref,
    ) = staged
    n = n_clump * n_group
    my_clump, my_group = lax.axis_index("clump"), lax.axis_index("grp")

    def ahead_of(mine, step, size):
        there = mine + step
        return jnp.where(there >= size, there - size, there)

    def behind(mine, step, size):
        there = mine - step
        return jnp.where(there < 0, there + size, there)

    def each_other(act, there):
        groups = [there(my_group, g, n_group) for g in range(n_group)]

        def row(c, first):
            clump = there(my_clump, c, n_clump)
            for g in range(first, n_group):
                act(c * n_group + g, (clump, groups[g]))

        row(0, 1)
        if n_clump <= 8:
            for c in range(1, n_clump):
                row(c, 0)
        else:

            @pl.loop(1, n_clump)
            def _(c):
                row(c, 0)

    barrier = pltpu.get_barrier_semaphore()

    def greet(block, device):
        pl.semaphore_signal(barrier, inc=1, device_id=device, device_id_type=MESH)

    each_other(greet, ahead_of)
    for load in loads:
        load.start()

    nv, patches = flux_ref.shape
    types = scale_ref.shape[0]
    cols = cwt_ref.shape[1]
    lus = lwt_ref.shape[1]
    cells = target_ref.shape[1]
    rows = n * stride

    loads[0].wait()
    target = target_ref[...]
    owner, local = split_by(target, cells)
    owner_b = jnp.broadcast_to(owner.astype(F32), (cells, cells))
    same = owner_b == owner_b.T
    earlier = iota((cells, cells), 0) < iota((cells, cells), 1)
    rank = jnp.sum(jnp.where(same & earlier, 1.0, 0.0), axis=0, keepdims=True).astype(jnp.int32)
    to_clump, to_group = split_by(owner, n_group)
    block = behind(to_clump, my_clump, n_clump) * n_group
    block = (block + behind(to_group, my_group, n_group)) * stride
    from_block = behind(my_clump, to_clump, n_clump) * n_group
    from_block = (from_block + behind(my_group, to_group, n_group)) * stride
    part, line = split_by(rank, half)
    slot_of = onehot(iota((2 * rows, cells), 0) == part * rows + block + line)

    loads[10].wait()
    frac = frac_ref[...]
    at = iota((rows, cells), 0)
    asks = jnp.where(at == block, (local + 1).astype(F32), 0.0).astype(BF16)
    ask_rows = dot_nt(asks, onehot(iota((128, cells), 0) == rank))
    second = split_by(iota((rows, 128), 0), stride)[1] == 1
    ask[...] = jnp.where(second, jnp.broadcast_to(frac, (rows, cells)), ask_rows)
    asked[0:2, :] = ask[0:2, :]
    for load in loads[1:5]:
        load.wait()
    def copy(source, into, k, count, block, device):
        start = block * stride
        lines = pl.ds(start if isinstance(start, int) else pl.multiple_of(start, stride), count)
        return pltpu.make_async_remote_copy(
            src_ref=source.at[lines],
            dst_ref=into.at[lines],
            send_sem=send_sem.at[k],
            recv_sem=recv_sem.at[k],
            device_id=device,
            device_id_type=MESH,
        )

    def send_all(source, into, k, count, there):
        def one(block, device):
            copy(source, into, k, count, block, device).start()

        each_other(one, there)

    def wait(buffer, sem, count):
        rest = buffer.at[pl.ds(0, (n - 1) * count)]
        pltpu.make_async_copy(rest, rest, sem).wait()

    lu_hi, lu_lo = halves(lwt_ref[...])
    lu_rows = rows_of([lu_hi, lu_lo, lgrid_ref[...]], 16)
    lu_of = onehot(iota((lus, cols), 0) == clu_ref[...])
    col_vals = dot(lu_rows, lu_of)
    col_w = cwt_ref[...] * (col_vals[0:1] + col_vals[1:2])
    pl.semaphore_wait(barrier, n - 1)
    send_all(ask, asked, 0, 2, ahead_of)

    for load in loads[5:7]:
        load.wait()
    c_hi, c_lo = halves(col_w)
    col_rows = rows_of([c_hi, c_lo, col_vals[2:3]], 16)
    col_of = onehot(iota((cols, patches), 0) == pcol_ref[...])
    patch_vals = dot(col_rows, col_of)
    alive = jnp.where(iota((1, patches), 1) < count_ref[0], 1.0, 0.0)
    weight = alive * pwt_ref[...] * (patch_vals[0:1] + patch_vals[1:2])
    home = patch_vals[2:3].astype(jnp.int32)
    home_of = onehot(iota((cells, patches), 0) == home)

    for load in loads[7:10]:
        load.wait()
    table = scale_ref[...]
    t1 = table.astype(BF16).astype(F32)
    t2 = (table - t1).astype(BF16).astype(F32)
    t3 = table - t1 - t2
    pad = 128 - 3 * types
    stacked = jnp.concatenate([t1, t2, t3, jnp.zeros((pad, nv), F32)], axis=0)
    stacked = jnp.concatenate([stacked, jnp.zeros((128, 128 - nv), F32)], axis=1)
    scale_t = stacked.T[:nv].astype(BF16)
    kind = iota((128, patches), 0)
    type_of = onehot(
        (kind == pft_ref[...])
        | (kind == pft_ref[...] + types)
        | (kind == pft_ref[...] + 2 * types)
    )
    scaled = flux_ref[...] * dot(scale_t, type_of)

    x_hi, x_lo = halves(scaled * weight)
    w_hi, w_lo = halves(weight)
    sums = dot_nt(
        jnp.concatenate([x_hi, x_lo, rows_of([w_hi, w_lo], 16)], axis=0), home_of
    )
    num = sums[:nv] + sums[nv : 2 * nv]
    den = sums[2 * nv : 2 * nv + 1] + sums[2 * nv + 1 : 2 * nv + 2]
    mean = num / jnp.maximum(den, 1.0)

    send[...] = pack(slot_of, mean)
    recv[0:half, :] = send[0:half, :]
    send_all(send, recv, 1, half, ahead_of)

    loads[11].wait()
    other = (1.0 - frac) * field_ref[...]
    lane = iota((2 * rows, 128), 0)
    lane_part = jnp.where(lane >= rows, 1, 0)
    lane_line = split_by(lane - lane_part * rows, stride)[1]
    its_lane = (lane_line < half) & (
        iota((2 * rows, 128), 1) == lane_part * half + lane_line
    )
    in_two = split_by(iota((rows, 128), 0), stride)[1] < 2
    in_half = split_by(iota((rows, 128), 0), stride)[1] < half
    wait(asked, recv_sem.at[0], 2)
    told = jnp.where(in_two, asked[...], 0.0)
    ids_of = jnp.broadcast_to(
        told.reshape(n, stride, 128)[:, 0:1, :], (n, stride, 128)
    ).reshape(rows, 128)
    spread = jnp.where(its_lane, jnp.concatenate([ids_of, ids_of], axis=0), 0.0).astype(BF16)
    ids = dot(spread, jnp.ones((128, cells), BF16))
    owned_of = onehot(ids == (iota((2 * rows, cells), 1) + 1).astype(F32))
    reply[...] = pack(owned_of, other)
    back[0:half, :] = reply[0:half, :]
    send_all(reply, back, 2, half, behind)

    all_frac = select(told.T, onehot(iota((rows, cells), 0) == from_block + 1))
    cell_frac = jnp.sum(
        jnp.where(iota((128, cells), 0) == local, all_frac, 0.0), axis=0, keepdims=True
    )
    land_part = cell_frac * mean

    wait(recv, recv_sem.at[1], half)
    owned = select(unpack(jnp.where(in_half, recv[...], 0.0)), owned_of)
    merged_ref[...] = frac * owned + other

    wait(back, recv_sem.at[2], half)
    cell = land_part + select(unpack(jnp.where(in_half, back[...], 0.0)), slot_of)
    anomaly_ref[...] = alive * (scaled - select(cell, home_of))
    wait(ask, send_sem.at[0], 2)
    wait(send, send_sem.at[1], half)
    wait(reply, send_sem.at[2], half)


def store_kernel(merged, anomaly, merged_out, anomaly_out, sem):
    stores = [
        pltpu.make_async_copy(merged, merged_out, sem.at[0]),
        pltpu.make_async_copy(anomaly, anomaly_out, sem.at[1]),
    ]
    for store in stores:
        store.start()
    for store in stores:
        store.wait()


def per_device(
    flux, patch_pft, patch_wt, patch_col, col_wt, col_lu, lu_wt, lu_grid, cell_target,
    patch_count, pft_scale, cpl_frac, cpl_field,
):
    n_clump = lax.axis_size("clump")
    n_group = lax.axis_size("grp")
    n = n_clump * n_group
    nv = flux.shape[2]
    patches = flux.shape[1]
    cells = cell_target.shape[1]
    cap = max(2, 2 * cells // n)
    half = -(-cap // 2)
    stride = -(-max(half, 2) // 8) * 8
    vmem = pl.BlockSpec(memory_space=pltpu.VMEM)
    hbm = pl.BlockSpec(memory_space=pltpu.HBM)
    buffer = pltpu.VMEM((n * stride, 128), F32)
    inputs = (
        cell_target, lu_wt, lu_grid, col_lu, col_wt, patch_col, patch_wt,
        pft_scale, patch_pft, flux[0].T, cpl_frac.reshape(1, -1), cpl_field.T,
    )
    shapes = (
        jax.ShapeDtypeStruct((nv, cells), F32),
        jax.ShapeDtypeStruct((nv, patches), F32),
    )
    results = pl.pallas_call(
        functools.partial(kernel, n_clump, n_group, cap, half, stride),
        out_shape=tuple(pltpu.VMEM(x.shape, x.dtype) for x in shapes),
        in_specs=[pl.BlockSpec(memory_space=pltpu.SMEM)] + [hbm] * INPUTS,
        out_specs=(vmem, vmem),
        scratch_shapes=[
            buffer, buffer, buffer, buffer, buffer, buffer,
            pltpu.SemaphoreType.DMA((3,)),
            pltpu.SemaphoreType.DMA((3,)),
            pltpu.SemaphoreType.DMA((INPUTS,)),
        ]
        + [
            pltpu.VMEM(x.shape, x.dtype)
            for x in inputs
        ],
        compiler_params=pltpu.CompilerParams(
            collective_id=0, has_side_effects=True, vmem_limit_bytes=48 * 1024 * 1024
        ),
    )(patch_count, *[pltpu.with_memory_space_constraint(x, pltpu.HBM) for x in inputs])
    merged, anomaly = pl.pallas_call(
        store_kernel,
        out_shape=shapes,
        in_specs=[vmem, vmem],
        out_specs=(hbm, hbm),
        scratch_shapes=[pltpu.SemaphoreType.DMA((2,))],
        compiler_params=pltpu.CompilerParams(vmem_limit_bytes=4 * 1024 * 1024),
    )(*results)
    return merged.T, anomaly.T[None]


def solution(mesh):
    split = P(("clump", "grp"))
    return jax.shard_map(
        per_device,
        mesh=mesh,
        in_specs=(split,) * 10 + (P(),) + (split,) * 2,
        out_specs=(split, split),
        check_vma=False,
    )
```

time: 26.1 us -> 19.7 us (0.75)
  Pallas kernels: 21.5 us -> 18.2 us
  local copies, waits for them, and re-layouts: 3.05 us -> 0 us
    pallas_call x1 -> x2, Pallas kernels: 21.5 us -> 18.2 us  [the longest x1 17.5 us: per_device(): pl.pallas_call(functools.partial(kernel, n_clump, n_group, cap, half, str...]
    unnamed x2 -> x0, local copies, waits for them, and re-layouts: 3.05 us -> none
where the time goes in v2:
time: 19.7 us; the launch traced here: 19.5 us
  Pallas kernels  18.2 us (92%)
  between operations  1.29 us (7%)
    pallas_call x1, Pallas kernels, per_device(): pl.pallas_call(functools.partial(kernel, n_clump, n_group, cap, half, str...  17.5 us
    pallas_call x1, Pallas kernels, per_device(): pl.pallas_call(store_kernel, out_shape=shapes, in_specs=[vmem, vmem], out...  0.73 us

profile of v2, /device:TPU:0, one launch (start us, length us, event | category | flops | bytes accessed | tf_op | source)
XLA Modules:
  0.0 19.5 jit_solution(18323764847359225401)
XLA Ops:
  1.3 17.5 %shard_map.140 = (f32[64,128]{1,0:T(8,128)S(1)}, f32[64,1024]{1,0:T(8,128)S(1)}) custom-call(s32[1]{0:T(128)S(6)} %copy.15.refs_0_, s32[1,128]{1,0:T(1,128)} %refs_1_.1, f32[1,256]{1,0:T(1,128)} %refs_2_.1, s32[1,256]{1,0:T(1,128)} %refs_3_.1, s32[1,512]{1,0:T(1,128)} %refs_4_.1, f32[1,512]{1,0:T(1,128)} %refs_5_.1, s32[1,1024]{1,0:T(1,128)} %refs_6_.1, ...), custom_call_target="tpu_custom_call" | custom-call | tf_op jit(solution)/shard_map/pallas_call | solution.py:311
  18.8 0.7 %shard_map.141 = (f32[64,128]{1,0:T(8,128)}, f32[64,1024]{1,0:T(8,128)}) custom-call(f32[64,128]{1,0:T(8,128)S(1)} %get-tuple-element.6.merged, f32[64,1024]{1,0:T(8,128)S(1)} %get-tuple-element.7.anomaly), custom_call_target="tpu_custom_call" | custom-call | tf_op jit(solution)/shard_map/pallas_call | solution.py:330
